TPU v7x, 32 devices: a 4x4x1 block of a 4x4x8 slice. The times are simulated.
32 devices in a mesh: batch: 1 (over z), cy: 4 (over y), cx: 8 (over x, core).
Axes of the slice: x: 4, y: 4, z: 1, core: 2. Of those that a mesh axis runs over, the one named last changes fastest.
The devices are a block of a 4x4x8 slice.
Arguments:
- q_seq: bfloat16 [8192, 14, 64], P(('batch', 'cx', 'cy'))
- k_seq: bfloat16 [8192, 2, 64], P(('batch', 'cx', 'cy'))
- v_seq: bfloat16 [8192, 2, 64], P(('batch', 'cx', 'cy'))
Outputs:
- output: bfloat16 [8192, 14, 64], P(('batch', 'cx', 'cy'))
All inputs are finite; a program needn't handle non-finite values.
Results may differ from a plain program's by a relative error of at most 0.00489606.
Values are sent between devices in bfloat16 or wider.
A program may use at most 768 MiB of HBM per device.

v0:
```python
import math
import jax
import jax.numpy as jnp
from jax import lax
from jax.sharding import PartitionSpec as P


def block_update(running, q_grouped, k_blk, v_blk):
    row_max, row_sum, out_acc = running
    score_scale = 1.0 / math.sqrt(q_grouped.shape[-1])
    scores = jnp.einsum("qkgd,skd->kgqs", q_grouped, k_blk, preferred_element_type=jnp.float32) * score_scale
    new_max = jnp.maximum(row_max, jnp.max(scores, axis=-1))
    rescale = jnp.exp(row_max - new_max)
    prob_blk = jnp.exp(scores - new_max[..., None])
    row_sum = row_sum * rescale + jnp.sum(prob_blk, axis=-1)
    weighted = jnp.einsum("kgqs,skd->kgqd", prob_blk.astype(jnp.bfloat16), v_blk, preferred_element_type=jnp.float32)
    out_acc = out_acc * rescale[..., None] + weighted
    return new_max, row_sum, out_acc


def start_state(q_grouped):
    tokens, num_kv, groups, head_dim = q_grouped.shape
    row_max = jnp.full((num_kv, groups, tokens), -jnp.inf, jnp.float32)
    row_sum = jnp.zeros((num_kv, groups, tokens), jnp.float32)
    out_acc = jnp.zeros((num_kv, groups, tokens, head_dim), jnp.float32)
    return row_max, row_sum, out_acc


def finish(running, tokens, num_heads, head_dim):
    row_max, row_sum, out_acc = running
    result = out_acc / row_sum[..., None]
    return jnp.transpose(result, (2, 0, 1, 3)).reshape(tokens, num_heads, head_dim).astype(jnp.bfloat16)


def solution(mesh):
    size_x = mesh.shape["cx"]
    size_y = mesh.shape["cy"]
    seq_spec = P(("batch", "cx", "cy"), None, None)
    perm_x = [(dev_idx, (dev_idx + 1) % size_x) for dev_idx in range(size_x)]
    perm_y = [(dev_idx, (dev_idx + 1) % size_y) for dev_idx in range(size_y)]

    def local_attention(q_local, k_local, v_local):
        tokens, num_heads, head_dim = q_local.shape
        num_kv = k_local.shape[1]
        q_grouped = q_local.reshape(tokens, num_kv, num_heads // num_kv, head_dim)

        def step_x(step_idx, loop_state):
            running, k_blk, v_blk = loop_state
            running = block_update(running, q_grouped, k_blk, v_blk)
            k_blk = lax.ppermute(k_blk, "cx", perm_x)
            v_blk = lax.ppermute(v_blk, "cx", perm_x)
            return running, k_blk, v_blk

        def sweep_x(loop_state):
            running, k_blk, v_blk = lax.fori_loop(0, size_x - 1, step_x, loop_state)
            return block_update(running, q_grouped, k_blk, v_blk), k_blk, v_blk

        def step_y(step_idx, loop_state):
            running, k_blk, v_blk = sweep_x(loop_state)
            k_blk = lax.ppermute(k_blk, "cy", perm_y)
            v_blk = lax.ppermute(v_blk, "cy", perm_y)
            return running, k_blk, v_blk

        loop_state = lax.fori_loop(0, size_y - 1, step_y, (start_state(q_grouped), k_local, v_local))
        running = sweep_x(loop_state)[0]
        return finish(running, tokens, num_heads, head_dim)

    return jax.shard_map(local_attention, mesh=mesh, in_specs=(seq_spec, seq_spec, seq_spec), out_specs=seq_spec, check_vma=False)
```

profile of v0, /device:TPU:96, one launch (start us, length us, event | category | flops | bytes accessed | tf_op | source)
XLA Modules:
  0.0 183.8 jit_solution(17469876840814839292)
XLA Ops:
  1.7 138.9 %while.58 = (s32[]{:T(128)}, f32[2,7,256]{2,1,0:T(8,128)S(1)}, f32[2,7,256]{2,1,0:T(8,128)S(1)}, f32[2,7,256,64]{2,3,1,0:T(8,128)S(1)}, bf16[256,2,64]{0,2,1:T(8...) while((s32[]{:T(128)}, f32[2,7,256]{2,1,0:T(8,128)S(1)}, ...), condition=%wide.region_7.0_spmd.clone, body=%wide.region_0.0_spmd.clone.sunk | while | flops 485610496 | bytes 30765484 | solution.py:64
  1.8 39.3 %while.59 = (s32[]{:T(128)}, f32[2,7,256]{2,1,0:T(8,128)S(1)}, f32[2,7,256]{2,1,0:T(8,128)S(1)}, f32[2,7,256,64]{2,3,1,0:T(8,128)S(1)}, bf16[256,2,64]{0,2,1:T(8...) while((s32[]{:T(128)}, f32[2,7,256]{2,1,0:T(8,128)S(1)}, ...), condition=%wide.region_4.0_spmd, body=%wide.region_1.0_spmd.sunk | while | flops 242686976 | bytes 14450853 | solution.py:55
  3.0 1.7 bitcast_reduce_fusion.9
  8.2 1.7 bitcast_reduce_fusion.9
  13.2 1.7 bitcast_reduce_fusion.9
  16.5 1.5 collective-permute-done.2
  18.8 1.7 bitcast_reduce_fusion.9
  24.4 1.7 bitcast_reduce_fusion.9
  30.0 1.7 bitcast_reduce_fusion.9
  33.3 1.5 collective-permute-done.2
  35.7 1.7 bitcast_reduce_fusion.9
  41.2 1.5 collective-permute-start.4
  42.7 2.1 %collective-permute-start.5 = (bf16[256,2,64]{0,2,1:T(8,128)(2,1)S(1)}, bf16[256,2,64]{0,2,1:T(8,128)(2,1)S(1)}, u32[]{:S(2)}, u32[]{:S(2)}) collective-permute-start(bf16[256,2,64]{0,2,1:T(8,128)(2,1)S(1)} %get-tuple-element.392), channel_id=1, source_target_pairs={{0,8},{8,16},{16,24},{24,0},{1,9},{9,17},{17,25},{25,1},{2,10},{10... | collective-permute-start | bytes 196616 | tf_op jit(solution)/shard_map/while/body/eval_jaxpr/ppermute | solution.py:61
  44.8 1.7 bitcast_reduce_fusion.8
  48.3 39.3 %while.59 = (s32[]{:T(128)}, f32[2,7,256]{2,1,0:T(8,128)S(1)}, f32[2,7,256]{2,1,0:T(8,128)S(1)}, f32[2,7,256,64]{2,3,1,0:T(8,128)S(1)}, bf16[256,2,64]{0,2,1:T(8...) while((s32[]{:T(128)}, f32[2,7,256]{2,1,0:T(8,128)S(1)}, ...), condition=%wide.region_4.0_spmd, body=%wide.region_1.0_spmd.sunk | while | flops 242686976 | bytes 14450853 | solution.py:55
  48.5 1.7 bitcast_reduce_fusion.9
  54.1 1.7 bitcast_reduce_fusion.9
  57.3 1.5 collective-permute-done.2
  59.7 1.7 bitcast_reduce_fusion.9
  65.3 1.7 bitcast_reduce_fusion.9
  68.6 1.5 collective-permute-done.2
  70.9 1.7 bitcast_reduce_fusion.9
  74.2 1.5 collective-permute-done.2
  76.5 1.7 bitcast_reduce_fusion.9
  82.1 1.7 bitcast_reduce_fusion.9
  85.4 1.5 collective-permute-done.2
  87.6 1.8 collective-permute-start.4
  90.4 1.7 bitcast_reduce_fusion.8
  95.0 39.3 %while.59 = (s32[]{:T(128)}, f32[2,7,256]{2,1,0:T(8,128)S(1)}, f32[2,7,256]{2,1,0:T(8,128)S(1)}, f32[2,7,256,64]{2,3,1,0:T(8,128)S(1)}, bf16[256,2,64]{0,2,1:T(8...) while((s32[]{:T(128)}, f32[2,7,256]{2,1,0:T(8,128)S(1)}, ...), condition=%wide.region_4.0_spmd, body=%wide.region_1.0_spmd.sunk | while | flops 242686976 | bytes 14450853 | solution.py:55
  95.2 1.7 bitcast_reduce_fusion.9
  100.8 1.7 bitcast_reduce_fusion.9
  106.4 1.7 bitcast_reduce_fusion.9
  112.0 1.7 bitcast_reduce_fusion.9
  115.3 1.5 collective-permute-done.2
  117.6 1.7 bitcast_reduce_fusion.9
  123.3 1.7 bitcast_reduce_fusion.9
  128.9 1.7 bitcast_reduce_fusion.9
  135.1 1.7 bitcast_reduce_fusion.8
  140.5 39.3 %while.56 = (s32[]{:T(128)}, f32[2,7,256]{2,1,0:T(8,128)S(1)}, f32[2,7,256]{2,1,0:T(8,128)S(1)}, f32[2,7,256,64]{2,3,1,0:T(8,128)S(1)}, bf16[256,2,64]{0,2,1:T(8...) while((s32[]{:T(128)}, f32[2,7,256]{2,1,0:T(8,128)S(1)}, ...), condition=%wide.region_11.0_spmd, body=%wide.region_8.0_spmd.sunk | while | flops 242686976 | bytes 14450853 | solution.py:55
  140.7 1.7 bitcast_reduce_fusion.7
  146.3 1.7 bitcast_reduce_fusion.7
  151.9 1.7 bitcast_reduce_fusion.7
  157.5 1.7 bitcast_reduce_fusion.7
  163.1 1.7 bitcast_reduce_fusion.7
  168.7 1.7 bitcast_reduce_fusion.7
  174.3 1.7 bitcast_reduce_fusion.7
  179.8 1.7 bitcast_reduce_fusion.3
  182.2 1.6 fusion.55
  (342 shorter events, 109.3 us)
Async XLA Ops:
  1.8 4.9 %collective-permute-start.2 = (bf16[256,2,64]{0,2,1:T(8,128)(2,1)S(1)}, bf16[256,2,64]{0,2,1:T(8,128)(2,1)S(1)}, u32[]{:S(2)}, u32[]{:S(2)}) collective-permute-start(bf16[256,2,64]{0,2,1:T(8,128)(2,1)S(1)} %copy.30), channel_id=1, source_target_pairs={{0,1},{1,2},{2,3},{3,4},{4,5},{5,6},{6,7},{7,0},{8,9},{9,10},{10,1... | collective-permute-start | bytes 196616 | tf_op jit(solution)/shard_map/while/body/eval_jaxpr/while/body/eval_jaxpr/ppermute | solution.py:50
  1.9 5.6 %collective-permute-start.3 = (bf16[256,2,64]{0,2,1:T(8,128)(2,1)S(1)}, bf16[256,2,64]{0,2,1:T(8,128)(2,1)S(1)}, u32[]{:S(2)}, u32[]{:S(2)}) collective-permute-start(bf16[256,2,64]{0,2,1:T(8,128)(2,1)S(1)} %copy.31), channel_id=1, source_target_pairs={{0,1},{1,2},{2,3},{3,4},{4,5},{5,6},{6,7},{7,0},{8,9},{9,10},{10,1... | collective-permute-start | bytes 196616 | tf_op jit(solution)/shard_map/while/body/eval_jaxpr/while/body/eval_jaxpr/ppermute | solution.py:51
  7.5 4.9 %collective-permute-start.2 = (bf16[256,2,64]{0,2,1:T(8,128)(2,1)S(1)}, bf16[256,2,64]{0,2,1:T(8,128)(2,1)S(1)}, u32[]{:S(2)}, u32[]{:S(2)}) collective-permute-start(bf16[256,2,64]{0,2,1:T(8,128)(2,1)S(1)} %copy.30), channel_id=1, source_target_pairs={{0,1},{1,2},{2,3},{3,4},{4,5},{5,6},{6,7},{7,0},{8,9},{9,10},{10,1... | collective-permute-start | bytes 196616 | tf_op jit(solution)/shard_map/while/body/eval_jaxpr/while/body/eval_jaxpr/ppermute | solution.py:50
  7.5 5.6 %collective-permute-start.3 = (bf16[256,2,64]{0,2,1:T(8,128)(2,1)S(1)}, bf16[256,2,64]{0,2,1:T(8,128)(2,1)S(1)}, u32[]{:S(2)}, u32[]{:S(2)}) collective-permute-start(bf16[256,2,64]{0,2,1:T(8,128)(2,1)S(1)} %copy.31), channel_id=1, source_target_pairs={{0,1},{1,2},{2,3},{3,4},{4,5},{5,6},{6,7},{7,0},{8,9},{9,10},{10,1... | collective-permute-start | bytes 196616 | tf_op jit(solution)/shard_map/while/body/eval_jaxpr/while/body/eval_jaxpr/ppermute | solution.py:51
  13.1 4.9 %collective-permute-start.2 = (bf16[256,2,64]{0,2,1:T(8,128)(2,1)S(1)}, bf16[256,2,64]{0,2,1:T(8,128)(2,1)S(1)}, u32[]{:S(2)}, u32[]{:S(2)}) collective-permute-start(bf16[256,2,64]{0,2,1:T(8,128)(2,1)S(1)} %copy.30), channel_id=1, source_target_pairs={{0,1},{1,2},{2,3},{3,4},{4,5},{5,6},{6,7},{7,0},{8,9},{9,10},{10,1... | collective-permute-start | bytes 196616 | tf_op jit(solution)/shard_map/while/body/eval_jaxpr/while/body/eval_jaxpr/ppermute | solution.py:50
  13.1 5.6 %collective-permute-start.3 = (bf16[256,2,64]{0,2,1:T(8,128)(2,1)S(1)}, bf16[256,2,64]{0,2,1:T(8,128)(2,1)S(1)}, u32[]{:S(2)}, u32[]{:S(2)}) collective-permute-start(bf16[256,2,64]{0,2,1:T(8,128)(2,1)S(1)} %copy.31), channel_id=1, source_target_pairs={{0,1},{1,2},{2,3},{3,4},{4,5},{5,6},{6,7},{7,0},{8,9},{9,10},{10,1... | collective-permute-start | bytes 196616 | tf_op jit(solution)/shard_map/while/body/eval_jaxpr/while/body/eval_jaxpr/ppermute | solution.py:51
  18.7 4.9 %collective-permute-start.2 = (bf16[256,2,64]{0,2,1:T(8,128)(2,1)S(1)}, bf16[256,2,64]{0,2,1:T(8,128)(2,1)S(1)}, u32[]{:S(2)}, u32[]{:S(2)}) collective-permute-start(bf16[256,2,64]{0,2,1:T(8,128)(2,1)S(1)} %copy.30), channel_id=1, source_target_pairs={{0,1},{1,2},{2,3},{3,4},{4,5},{5,6},{6,7},{7,0},{8,9},{9,10},{10,1... | collective-permute-start | bytes 196616 | tf_op jit(solution)/shard_map/while/body/eval_jaxpr/while/body/eval_jaxpr/ppermute | solution.py:50
  18.8 5.6 %collective-permute-start.3 = (bf16[256,2,64]{0,2,1:T(8,128)(2,1)S(1)}, bf16[256,2,64]{0,2,1:T(8,128)(2,1)S(1)}, u32[]{:S(2)}, u32[]{:S(2)}) collective-permute-start(bf16[256,2,64]{0,2,1:T(8,128)(2,1)S(1)} %copy.31), channel_id=1, source_target_pairs={{0,1},{1,2},{2,3},{3,4},{4,5},{5,6},{6,7},{7,0},{8,9},{9,10},{10,1... | collective-permute-start | bytes 196616 | tf_op jit(solution)/shard_map/while/body/eval_jaxpr/while/body/eval_jaxpr/ppermute | solution.py:51
  24.3 4.9 %collective-permute-start.2 = (bf16[256,2,64]{0,2,1:T(8,128)(2,1)S(1)}, bf16[256,2,64]{0,2,1:T(8,128)(2,1)S(1)}, u32[]{:S(2)}, u32[]{:S(2)}) collective-permute-start(bf16[256,2,64]{0,2,1:T(8,128)(2,1)S(1)} %copy.30), channel_id=1, source_target_pairs={{0,1},{1,2},{2,3},{3,4},{4,5},{5,6},{6,7},{7,0},{8,9},{9,10},{10,1... | collective-permute-start | bytes 196616 | tf_op jit(solution)/shard_map/while/body/eval_jaxpr/while/body/eval_jaxpr/ppermute | solution.py:50
  24.4 5.6 %collective-permute-start.3 = (bf16[256,2,64]{0,2,1:T(8,128)(2,1)S(1)}, bf16[256,2,64]{0,2,1:T(8,128)(2,1)S(1)}, u32[]{:S(2)}, u32[]{:S(2)}) collective-permute-start(bf16[256,2,64]{0,2,1:T(8,128)(2,1)S(1)} %copy.31), channel_id=1, source_target_pairs={{0,1},{1,2},{2,3},{3,4},{4,5},{5,6},{6,7},{7,0},{8,9},{9,10},{10,1... | collective-permute-start | bytes 196616 | tf_op jit(solution)/shard_map/while/body/eval_jaxpr/while/body/eval_jaxpr/ppermute | solution.py:51
  29.9 4.9 %collective-permute-start.2 = (bf16[256,2,64]{0,2,1:T(8,128)(2,1)S(1)}, bf16[256,2,64]{0,2,1:T(8,128)(2,1)S(1)}, u32[]{:S(2)}, u32[]{:S(2)}) collective-permute-start(bf16[256,2,64]{0,2,1:T(8,128)(2,1)S(1)} %copy.30), channel_id=1, source_target_pairs={{0,1},{1,2},{2,3},{3,4},{4,5},{5,6},{6,7},{7,0},{8,9},{9,10},{10,1... | collective-permute-start | bytes 196616 | tf_op jit(solution)/shard_map/while/body/eval_jaxpr/while/body/eval_jaxpr/ppermute | solution.py:50
  30.0 5.6 %collective-permute-start.3 = (bf16[256,2,64]{0,2,1:T(8,128)(2,1)S(1)}, bf16[256,2,64]{0,2,1:T(8,128)(2,1)S(1)}, u32[]{:S(2)}, u32[]{:S(2)}) collective-permute-start(bf16[256,2,64]{0,2,1:T(8,128)(2,1)S(1)} %copy.31), channel_id=1, source_target_pairs={{0,1},{1,2},{2,3},{3,4},{4,5},{5,6},{6,7},{7,0},{8,9},{9,10},{10,1... | collective-permute-start | bytes 196616 | tf_op jit(solution)/shard_map/while/body/eval_jaxpr/while/body/eval_jaxpr/ppermute | solution.py:51
  35.5 4.9 %collective-permute-start.2 = (bf16[256,2,64]{0,2,1:T(8,128)(2,1)S(1)}, bf16[256,2,64]{0,2,1:T(8,128)(2,1)S(1)}, u32[]{:S(2)}, u32[]{:S(2)}) collective-permute-start(bf16[256,2,64]{0,2,1:T(8,128)(2,1)S(1)} %copy.30), channel_id=1, source_target_pairs={{0,1},{1,2},{2,3},{3,4},{4,5},{5,6},{6,7},{7,0},{8,9},{9,10},{10,1... | collective-permute-start | bytes 196616 | tf_op jit(solution)/shard_map/while/body/eval_jaxpr/while/body/eval_jaxpr/ppermute | solution.py:50
  35.6 5.6 %collective-permute-start.3 = (bf16[256,2,64]{0,2,1:T(8,128)(2,1)S(1)}, bf16[256,2,64]{0,2,1:T(8,128)(2,1)S(1)}, u32[]{:S(2)}, u32[]{:S(2)}) collective-permute-start(bf16[256,2,64]{0,2,1:T(8,128)(2,1)S(1)} %copy.31), channel_id=1, source_target_pairs={{0,1},{1,2},{2,3},{3,4},{4,5},{5,6},{6,7},{7,0},{8,9},{9,10},{10,1... | collective-permute-start | bytes 196616 | tf_op jit(solution)/shard_map/while/body/eval_jaxpr/while/body/eval_jaxpr/ppermute | solution.py:51
  41.2 6.9 %collective-permute-start.4 = (bf16[256,2,64]{0,2,1:T(8,128)(2,1)S(1)}, bf16[256,2,64]{0,2,1:T(8,128)(2,1)S(1)}, u32[]{:S(2)}, u32[]{:S(2)}) collective-permute-start(bf16[256,2,64]{0,2,1:T(8,128)(2,1)S(1)} %get-tuple-element.391), channel_id=1, source_target_pairs={{0,8},{8,16},{16,24},{24,0},{1,9},{9,17},{17,25},{25,1},{2,10},{10... | collective-permute-start | bytes 196616 | tf_op jit(solution)/shard_map/while/body/eval_jaxpr/ppermute | solution.py:60
  42.7 5.5 %collective-permute-start.5 = (bf16[256,2,64]{0,2,1:T(8,128)(2,1)S(1)}, bf16[256,2,64]{0,2,1:T(8,128)(2,1)S(1)}, u32[]{:S(2)}, u32[]{:S(2)}) collective-permute-start(bf16[256,2,64]{0,2,1:T(8,128)(2,1)S(1)} %get-tuple-element.392), channel_id=1, source_target_pairs={{0,8},{8,16},{16,24},{24,0},{1,9},{9,17},{17,25},{25,1},{2,10},{10... | collective-permute-start | bytes 196616 | tf_op jit(solution)/shard_map/while/body/eval_jaxpr/ppermute | solution.py:61
  48.3 4.9 %collective-permute-start.2 = (bf16[256,2,64]{0,2,1:T(8,128)(2,1)S(1)}, bf16[256,2,64]{0,2,1:T(8,128)(2,1)S(1)}, u32[]{:S(2)}, u32[]{:S(2)}) collective-permute-start(bf16[256,2,64]{0,2,1:T(8,128)(2,1)S(1)} %copy.30), channel_id=1, source_target_pairs={{0,1},{1,2},{2,3},{3,4},{4,5},{5,6},{6,7},{7,0},{8,9},{9,10},{10,1... | collective-permute-start | bytes 196616 | tf_op jit(solution)/shard_map/while/body/eval_jaxpr/while/body/eval_jaxpr/ppermute | solution.py:50
  48.4 5.6 %collective-permute-start.3 = (bf16[256,2,64]{0,2,1:T(8,128)(2,1)S(1)}, bf16[256,2,64]{0,2,1:T(8,128)(2,1)S(1)}, u32[]{:S(2)}, u32[]{:S(2)}) collective-permute-start(bf16[256,2,64]{0,2,1:T(8,128)(2,1)S(1)} %copy.31), channel_id=1, source_target_pairs={{0,1},{1,2},{2,3},{3,4},{4,5},{5,6},{6,7},{7,0},{8,9},{9,10},{10,1... | collective-permute-start | bytes 196616 | tf_op jit(solution)/shard_map/while/body/eval_jaxpr/while/body/eval_jaxpr/ppermute | solution.py:51
  54.0 4.9 %collective-permute-start.2 = (bf16[256,2,64]{0,2,1:T(8,128)(2,1)S(1)}, bf16[256,2,64]{0,2,1:T(8,128)(2,1)S(1)}, u32[]{:S(2)}, u32[]{:S(2)}) collective-permute-start(bf16[256,2,64]{0,2,1:T(8,128)(2,1)S(1)} %copy.30), channel_id=1, source_target_pairs={{0,1},{1,2},{2,3},{3,4},{4,5},{5,6},{6,7},{7,0},{8,9},{9,10},{10,1... | collective-permute-start | bytes 196616 | tf_op jit(solution)/shard_map/while/body/eval_jaxpr/while/body/eval_jaxpr/ppermute | solution.py:50
  54.0 5.6 %collective-permute-start.3 = (bf16[256,2,64]{0,2,1:T(8,128)(2,1)S(1)}, bf16[256,2,64]{0,2,1:T(8,128)(2,1)S(1)}, u32[]{:S(2)}, u32[]{:S(2)}) collective-permute-start(bf16[256,2,64]{0,2,1:T(8,128)(2,1)S(1)} %copy.31), channel_id=1, source_target_pairs={{0,1},{1,2},{2,3},{3,4},{4,5},{5,6},{6,7},{7,0},{8,9},{9,10},{10,1... | collective-permute-start | bytes 196616 | tf_op jit(solution)/shard_map/while/body/eval_jaxpr/while/body/eval_jaxpr/ppermute | solution.py:51
  59.6 4.9 %collective-permute-start.2 = (bf16[256,2,64]{0,2,1:T(8,128)(2,1)S(1)}, bf16[256,2,64]{0,2,1:T(8,128)(2,1)S(1)}, u32[]{:S(2)}, u32[]{:S(2)}) collective-permute-start(bf16[256,2,64]{0,2,1:T(8,128)(2,1)S(1)} %copy.30), channel_id=1, source_target_pairs={{0,1},{1,2},{2,3},{3,4},{4,5},{5,6},{6,7},{7,0},{8,9},{9,10},{10,1... | collective-permute-start | bytes 196616 | tf_op jit(solution)/shard_map/while/body/eval_jaxpr/while/body/eval_jaxpr/ppermute | solution.py:50
  59.6 5.6 %collective-permute-start.3 = (bf16[256,2,64]{0,2,1:T(8,128)(2,1)S(1)}, bf16[256,2,64]{0,2,1:T(8,128)(2,1)S(1)}, u32[]{:S(2)}, u32[]{:S(2)}) collective-permute-start(bf16[256,2,64]{0,2,1:T(8,128)(2,1)S(1)} %copy.31), channel_id=1, source_target_pairs={{0,1},{1,2},{2,3},{3,4},{4,5},{5,6},{6,7},{7,0},{8,9},{9,10},{10,1... | collective-permute-start | bytes 196616 | tf_op jit(solution)/shard_map/while/body/eval_jaxpr/while/body/eval_jaxpr/ppermute | solution.py:51
  65.2 4.9 %collective-permute-start.2 = (bf16[256,2,64]{0,2,1:T(8,128)(2,1)S(1)}, bf16[256,2,64]{0,2,1:T(8,128)(2,1)S(1)}, u32[]{:S(2)}, u32[]{:S(2)}) collective-permute-start(bf16[256,2,64]{0,2,1:T(8,128)(2,1)S(1)} %copy.30), channel_id=1, source_target_pairs={{0,1},{1,2},{2,3},{3,4},{4,5},{5,6},{6,7},{7,0},{8,9},{9,10},{10,1... | collective-permute-start | bytes 196616 | tf_op jit(solution)/shard_map/while/body/eval_jaxpr/while/body/eval_jaxpr/ppermute | solution.py:50
  65.2 5.6 %collective-permute-start.3 = (bf16[256,2,64]{0,2,1:T(8,128)(2,1)S(1)}, bf16[256,2,64]{0,2,1:T(8,128)(2,1)S(1)}, u32[]{:S(2)}, u32[]{:S(2)}) collective-permute-start(bf16[256,2,64]{0,2,1:T(8,128)(2,1)S(1)} %copy.31), channel_id=1, source_target_pairs={{0,1},{1,2},{2,3},{3,4},{4,5},{5,6},{6,7},{7,0},{8,9},{9,10},{10,1... | collective-permute-start | bytes 196616 | tf_op jit(solution)/shard_map/while/body/eval_jaxpr/while/body/eval_jaxpr/ppermute | solution.py:51
  70.8 4.9 %collective-permute-start.2 = (bf16[256,2,64]{0,2,1:T(8,128)(2,1)S(1)}, bf16[256,2,64]{0,2,1:T(8,128)(2,1)S(1)}, u32[]{:S(2)}, u32[]{:S(2)}) collective-permute-start(bf16[256,2,64]{0,2,1:T(8,128)(2,1)S(1)} %copy.30), channel_id=1, source_target_pairs={{0,1},{1,2},{2,3},{3,4},{4,5},{5,6},{6,7},{7,0},{8,9},{9,10},{10,1... | collective-permute-start | bytes 196616 | tf_op jit(solution)/shard_map/while/body/eval_jaxpr/while/body/eval_jaxpr/ppermute | solution.py:50
  70.8 5.6 %collective-permute-start.3 = (bf16[256,2,64]{0,2,1:T(8,128)(2,1)S(1)}, bf16[256,2,64]{0,2,1:T(8,128)(2,1)S(1)}, u32[]{:S(2)}, u32[]{:S(2)}) collective-permute-start(bf16[256,2,64]{0,2,1:T(8,128)(2,1)S(1)} %copy.31), channel_id=1, source_target_pairs={{0,1},{1,2},{2,3},{3,4},{4,5},{5,6},{6,7},{7,0},{8,9},{9,10},{10,1... | collective-permute-start | bytes 196616 | tf_op jit(solution)/shard_map/while/body/eval_jaxpr/while/body/eval_jaxpr/ppermute | solution.py:51
  76.4 4.9 %collective-permute-start.2 = (bf16[256,2,64]{0,2,1:T(8,128)(2,1)S(1)}, bf16[256,2,64]{0,2,1:T(8,128)(2,1)S(1)}, u32[]{:S(2)}, u32[]{:S(2)}) collective-permute-start(bf16[256,2,64]{0,2,1:T(8,128)(2,1)S(1)} %copy.30), channel_id=1, source_target_pairs={{0,1},{1,2},{2,3},{3,4},{4,5},{5,6},{6,7},{7,0},{8,9},{9,10},{10,1... | collective-permute-start | bytes 196616 | tf_op jit(solution)/shard_map/while/body/eval_jaxpr/while/body/eval_jaxpr/ppermute | solution.py:50
  76.4 5.6 %collective-permute-start.3 = (bf16[256,2,64]{0,2,1:T(8,128)(2,1)S(1)}, bf16[256,2,64]{0,2,1:T(8,128)(2,1)S(1)}, u32[]{:S(2)}, u32[]{:S(2)}) collective-permute-start(bf16[256,2,64]{0,2,1:T(8,128)(2,1)S(1)} %copy.31), channel_id=1, source_target_pairs={{0,1},{1,2},{2,3},{3,4},{4,5},{5,6},{6,7},{7,0},{8,9},{9,10},{10,1... | collective-permute-start | bytes 196616 | tf_op jit(solution)/shard_map/while/body/eval_jaxpr/while/body/eval_jaxpr/ppermute | solution.py:51
  82.0 5.6 %collective-permute-start.3 = (bf16[256,2,64]{0,2,1:T(8,128)(2,1)S(1)}, bf16[256,2,64]{0,2,1:T(8,128)(2,1)S(1)}, u32[]{:S(2)}, u32[]{:S(2)}) collective-permute-start(bf16[256,2,64]{0,2,1:T(8,128)(2,1)S(1)} %copy.31), channel_id=1, source_target_pairs={{0,1},{1,2},{2,3},{3,4},{4,5},{5,6},{6,7},{7,0},{8,9},{9,10},{10,1... | collective-permute-start | bytes 196616 | tf_op jit(solution)/shard_map/while/body/eval_jaxpr/while/body/eval_jaxpr/ppermute | solution.py:51
  87.6 6.0 %collective-permute-start.4 = (bf16[256,2,64]{0,2,1:T(8,128)(2,1)S(1)}, bf16[256,2,64]{0,2,1:T(8,128)(2,1)S(1)}, u32[]{:S(2)}, u32[]{:S(2)}) collective-permute-start(bf16[256,2,64]{0,2,1:T(8,128)(2,1)S(1)} %get-tuple-element.391), channel_id=1, source_target_pairs={{0,8},{8,16},{16,24},{24,0},{1,9},{9,17},{17,25},{25,1},{2,10},{10... | collective-permute-start | bytes 196616 | tf_op jit(solution)/shard_map/while/body/eval_jaxpr/ppermute | solution.py:60
  89.4 5.5 %collective-permute-start.5 = (bf16[256,2,64]{0,2,1:T(8,128)(2,1)S(1)}, bf16[256,2,64]{0,2,1:T(8,128)(2,1)S(1)}, u32[]{:S(2)}, u32[]{:S(2)}) collective-permute-start(bf16[256,2,64]{0,2,1:T(8,128)(2,1)S(1)} %get-tuple-element.392), channel_id=1, source_target_pairs={{0,8},{8,16},{16,24},{24,0},{1,9},{9,17},{17,25},{25,1},{2,10},{10... | collective-permute-start | bytes 196616 | tf_op jit(solution)/shard_map/while/body/eval_jaxpr/ppermute | solution.py:61
  95.1 4.9 %collective-permute-start.2 = (bf16[256,2,64]{0,2,1:T(8,128)(2,1)S(1)}, bf16[256,2,64]{0,2,1:T(8,128)(2,1)S(1)}, u32[]{:S(2)}, u32[]{:S(2)}) collective-permute-start(bf16[256,2,64]{0,2,1:T(8,128)(2,1)S(1)} %copy.30), channel_id=1, source_target_pairs={{0,1},{1,2},{2,3},{3,4},{4,5},{5,6},{6,7},{7,0},{8,9},{9,10},{10,1... | collective-permute-start | bytes 196616 | tf_op jit(solution)/shard_map/while/body/eval_jaxpr/while/body/eval_jaxpr/ppermute | solution.py:50
  95.1 5.6 %collective-permute-start.3 = (bf16[256,2,64]{0,2,1:T(8,128)(2,1)S(1)}, bf16[256,2,64]{0,2,1:T(8,128)(2,1)S(1)}, u32[]{:S(2)}, u32[]{:S(2)}) collective-permute-start(bf16[256,2,64]{0,2,1:T(8,128)(2,1)S(1)} %copy.31), channel_id=1, source_target_pairs={{0,1},{1,2},{2,3},{3,4},{4,5},{5,6},{6,7},{7,0},{8,9},{9,10},{10,1... | collective-permute-start | bytes 196616 | tf_op jit(solution)/shard_map/while/body/eval_jaxpr/while/body/eval_jaxpr/ppermute | solution.py:51
  100.7 5.6 %collective-permute-start.3 = (bf16[256,2,64]{0,2,1:T(8,128)(2,1)S(1)}, bf16[256,2,64]{0,2,1:T(8,128)(2,1)S(1)}, u32[]{:S(2)}, u32[]{:S(2)}) collective-permute-start(bf16[256,2,64]{0,2,1:T(8,128)(2,1)S(1)} %copy.31), channel_id=1, source_target_pairs={{0,1},{1,2},{2,3},{3,4},{4,5},{5,6},{6,7},{7,0},{8,9},{9,10},{10,1... | collective-permute-start | bytes 196616 | tf_op jit(solution)/shard_map/while/body/eval_jaxpr/while/body/eval_jaxpr/ppermute | solution.py:51
  106.4 5.6 %collective-permute-start.3 = (bf16[256,2,64]{0,2,1:T(8,128)(2,1)S(1)}, bf16[256,2,64]{0,2,1:T(8,128)(2,1)S(1)}, u32[]{:S(2)}, u32[]{:S(2)}) collective-permute-start(bf16[256,2,64]{0,2,1:T(8,128)(2,1)S(1)} %copy.31), channel_id=1, source_target_pairs={{0,1},{1,2},{2,3},{3,4},{4,5},{5,6},{6,7},{7,0},{8,9},{9,10},{10,1... | collective-permute-start | bytes 196616 | tf_op jit(solution)/shard_map/while/body/eval_jaxpr/while/body/eval_jaxpr/ppermute | solution.py:51
  112.0 5.6 %collective-permute-start.3 = (bf16[256,2,64]{0,2,1:T(8,128)(2,1)S(1)}, bf16[256,2,64]{0,2,1:T(8,128)(2,1)S(1)}, u32[]{:S(2)}, u32[]{:S(2)}) collective-permute-start(bf16[256,2,64]{0,2,1:T(8,128)(2,1)S(1)} %copy.31), channel_id=1, source_target_pairs={{0,1},{1,2},{2,3},{3,4},{4,5},{5,6},{6,7},{7,0},{8,9},{9,10},{10,1... | collective-permute-start | bytes 196616 | tf_op jit(solution)/shard_map/while/body/eval_jaxpr/while/body/eval_jaxpr/ppermute | solution.py:51
  117.6 5.6 %collective-permute-start.3 = (bf16[256,2,64]{0,2,1:T(8,128)(2,1)S(1)}, bf16[256,2,64]{0,2,1:T(8,128)(2,1)S(1)}, u32[]{:S(2)}, u32[]{:S(2)}) collective-permute-start(bf16[256,2,64]{0,2,1:T(8,128)(2,1)S(1)} %copy.31), channel_id=1, source_target_pairs={{0,1},{1,2},{2,3},{3,4},{4,5},{5,6},{6,7},{7,0},{8,9},{9,10},{10,1... | collective-permute-start | bytes 196616 | tf_op jit(solution)/shard_map/while/body/eval_jaxpr/while/body/eval_jaxpr/ppermute | solution.py:51
  123.2 5.6 %collective-permute-start.3 = (bf16[256,2,64]{0,2,1:T(8,128)(2,1)S(1)}, bf16[256,2,64]{0,2,1:T(8,128)(2,1)S(1)}, u32[]{:S(2)}, u32[]{:S(2)}) collective-permute-start(bf16[256,2,64]{0,2,1:T(8,128)(2,1)S(1)} %copy.31), channel_id=1, source_target_pairs={{0,1},{1,2},{2,3},{3,4},{4,5},{5,6},{6,7},{7,0},{8,9},{9,10},{10,1... | collective-permute-start | bytes 196616 | tf_op jit(solution)/shard_map/while/body/eval_jaxpr/while/body/eval_jaxpr/ppermute | solution.py:51
  128.8 5.6 %collective-permute-start.3 = (bf16[256,2,64]{0,2,1:T(8,128)(2,1)S(1)}, bf16[256,2,64]{0,2,1:T(8,128)(2,1)S(1)}, u32[]{:S(2)}, u32[]{:S(2)}) collective-permute-start(bf16[256,2,64]{0,2,1:T(8,128)(2,1)S(1)} %copy.31), channel_id=1, source_target_pairs={{0,1},{1,2},{2,3},{3,4},{4,5},{5,6},{6,7},{7,0},{8,9},{9,10},{10,1... | collective-permute-start | bytes 196616 | tf_op jit(solution)/shard_map/while/body/eval_jaxpr/while/body/eval_jaxpr/ppermute | solution.py:51
  134.4 5.5 %collective-permute-start.4 = (bf16[256,2,64]{0,2,1:T(8,128)(2,1)S(1)}, bf16[256,2,64]{0,2,1:T(8,128)(2,1)S(1)}, u32[]{:S(2)}, u32[]{:S(2)}) collective-permute-start(bf16[256,2,64]{0,2,1:T(8,128)(2,1)S(1)} %get-tuple-element.391), channel_id=1, source_target_pairs={{0,8},{8,16},{16,24},{24,0},{1,9},{9,17},{17,25},{25,1},{2,10},{10... | collective-permute-start | bytes 196616 | tf_op jit(solution)/shard_map/while/body/eval_jaxpr/ppermute | solution.py:60
  134.4 6.2 %collective-permute-start.5 = (bf16[256,2,64]{0,2,1:T(8,128)(2,1)S(1)}, bf16[256,2,64]{0,2,1:T(8,128)(2,1)S(1)}, u32[]{:S(2)}, u32[]{:S(2)}) collective-permute-start(bf16[256,2,64]{0,2,1:T(8,128)(2,1)S(1)} %get-tuple-element.392), channel_id=1, source_target_pairs={{0,8},{8,16},{16,24},{24,0},{1,9},{9,17},{17,25},{25,1},{2,10},{10... | collective-permute-start | bytes 196616 | tf_op jit(solution)/shard_map/while/body/eval_jaxpr/ppermute | solution.py:61
  140.6 5.6 %collective-permute-start.1 = (bf16[256,2,64]{0,2,1:T(8,128)(2,1)S(1)}, bf16[256,2,64]{0,2,1:T(8,128)(2,1)S(1)}, u32[]{:S(2)}, u32[]{:S(2)}) collective-permute-start(bf16[256,2,64]{0,2,1:T(8,128)(2,1)S(1)} %copy.67), channel_id=1, source_target_pairs={{0,1},{1,2},{2,3},{3,4},{4,5},{5,6},{6,7},{7,0},{8,9},{9,10},{10,1... | collective-permute-start | bytes 196616 | tf_op jit(solution)/shard_map/while/body/eval_jaxpr/ppermute | solution.py:51
  146.2 5.6 %collective-permute-start.1 = (bf16[256,2,64]{0,2,1:T(8,128)(2,1)S(1)}, bf16[256,2,64]{0,2,1:T(8,128)(2,1)S(1)}, u32[]{:S(2)}, u32[]{:S(2)}) collective-permute-start(bf16[256,2,64]{0,2,1:T(8,128)(2,1)S(1)} %copy.67), channel_id=1, source_target_pairs={{0,1},{1,2},{2,3},{3,4},{4,5},{5,6},{6,7},{7,0},{8,9},{9,10},{10,1... | collective-permute-start | bytes 196616 | tf_op jit(solution)/shard_map/while/body/eval_jaxpr/ppermute | solution.py:51
  151.8 5.6 %collective-permute-start.1 = (bf16[256,2,64]{0,2,1:T(8,128)(2,1)S(1)}, bf16[256,2,64]{0,2,1:T(8,128)(2,1)S(1)}, u32[]{:S(2)}, u32[]{:S(2)}) collective-permute-start(bf16[256,2,64]{0,2,1:T(8,128)(2,1)S(1)} %copy.67), channel_id=1, source_target_pairs={{0,1},{1,2},{2,3},{3,4},{4,5},{5,6},{6,7},{7,0},{8,9},{9,10},{10,1... | collective-permute-start | bytes 196616 | tf_op jit(solution)/shard_map/while/body/eval_jaxpr/ppermute | solution.py:51
  157.4 5.6 %collective-permute-start.1 = (bf16[256,2,64]{0,2,1:T(8,128)(2,1)S(1)}, bf16[256,2,64]{0,2,1:T(8,128)(2,1)S(1)}, u32[]{:S(2)}, u32[]{:S(2)}) collective-permute-start(bf16[256,2,64]{0,2,1:T(8,128)(2,1)S(1)} %copy.67), channel_id=1, source_target_pairs={{0,1},{1,2},{2,3},{3,4},{4,5},{5,6},{6,7},{7,0},{8,9},{9,10},{10,1... | collective-permute-start | bytes 196616 | tf_op jit(solution)/shard_map/while/body/eval_jaxpr/ppermute | solution.py:51
  163.0 5.6 %collective-permute-start.1 = (bf16[256,2,64]{0,2,1:T(8,128)(2,1)S(1)}, bf16[256,2,64]{0,2,1:T(8,128)(2,1)S(1)}, u32[]{:S(2)}, u32[]{:S(2)}) collective-permute-start(bf16[256,2,64]{0,2,1:T(8,128)(2,1)S(1)} %copy.67), channel_id=1, source_target_pairs={{0,1},{1,2},{2,3},{3,4},{4,5},{5,6},{6,7},{7,0},{8,9},{9,10},{10,1... | collective-permute-start | bytes 196616 | tf_op jit(solution)/shard_map/while/body/eval_jaxpr/ppermute | solution.py:51
  168.6 5.6 %collective-permute-start.1 = (bf16[256,2,64]{0,2,1:T(8,128)(2,1)S(1)}, bf16[256,2,64]{0,2,1:T(8,128)(2,1)S(1)}, u32[]{:S(2)}, u32[]{:S(2)}) collective-permute-start(bf16[256,2,64]{0,2,1:T(8,128)(2,1)S(1)} %copy.67), channel_id=1, source_target_pairs={{0,1},{1,2},{2,3},{3,4},{4,5},{5,6},{6,7},{7,0},{8,9},{9,10},{10,1... | collective-permute-start | bytes 196616 | tf_op jit(solution)/shard_map/while/body/eval_jaxpr/ppermute | solution.py:51
  174.2 5.6 %collective-permute-start.1 = (bf16[256,2,64]{0,2,1:T(8,128)(2,1)S(1)}, bf16[256,2,64]{0,2,1:T(8,128)(2,1)S(1)}, u32[]{:S(2)}, u32[]{:S(2)}) collective-permute-start(bf16[256,2,64]{0,2,1:T(8,128)(2,1)S(1)} %copy.67), channel_id=1, source_target_pairs={{0,1},{1,2},{2,3},{3,4},{4,5},{5,6},{6,7},{7,0},{8,9},{9,10},{10,1... | collective-permute-start | bytes 196616 | tf_op jit(solution)/shard_map/while/body/eval_jaxpr/ppermute | solution.py:51
  (14 other events, 68.6 us)
where the time goes:
time: 185 us; the launch traced here: 184 us
  matrix products  83.4 us (45%)
  waiting for transfers between devices  63.8 us (34%)
  other arithmetic  21.1 us (11%)
  starting transfers between devices  11 us (6%)
  loops' own time  2.38 us (1%)
  local copies, waits for them, and re-layouts  2.13 us (1%)
    dot_general x32, matrix products, block_update(): jnp.einsum('qkgd,skd->kgqs', q_grouped, k_blk, preferred_element_type=jnp...  54.5 us
    ppermute x28, waiting for transfers between devices, step_x(): k_blk = lax.ppermute(k_blk, 'cx', perm_x)  40.7 us
    dot_general x32, matrix products, block_update(): jnp.einsum('kgqs,skd->kgqd', prob_blk.astype(jnp.bfloat16), v_blk, prefer...  28.9 us
    reduce_sum x32, other arithmetic, block_update(): row_sum = row_sum * rescale + jnp.sum(prob_blk, axis=-1)  20.2 us
    ppermute x28, waiting for transfers between devices, step_x(): v_blk = lax.ppermute(v_blk, 'cx', perm_x)  19.7 us
    ppermute x3, starting transfers between devices, step_y(): v_blk = lax.ppermute(v_blk, 'cy', perm_y)  3.75 us
  transfers between devices with their start and end apart: 62, of which 59 were waited for; matrix products, arithmetic and copies ran while one was open for 55% of the time, Pallas kernels for 0%

commit v1 on v0

v1 whole, which is shorter than its diff:
```python
import functools
import math
import jax
import jax.numpy as jnp
from jax import lax
from jax.experimental import pallas as pl
from jax.experimental.pallas import tpu as pltpu
from jax.sharding import PartitionSpec as P

SLOTS = [(0, 0), (1, 0), (-1, 0), (0, 1), (0, -1), (1, 1), (1, -1), (-1, 1), (-1, -1), (2, 0), (0, 2),
         (2, 1), (2, -1), (1, 2), (-1, 2), (2, 2)]
SLOT_OF = {offset: slot for slot, offset in enumerate(SLOTS)}
LAG = 2


def wrap(step):
    return (step + 1) % 4 - 1


def send_plan():
    plan = {}

    def add(what, offset, step_x, step_y):
        plan.setdefault((what, SLOT_OF[offset]), []).append((step_x, step_y))

    for what, swap in (("k", False), ("v", True)):
        flip = (lambda pair: (pair[1], pair[0])) if swap else (lambda pair: pair)
        sign = -1 if swap else 1

        def hop(offset, step):
            add(what, flip(offset), *flip(step))

        hop((0, 0), (1, 0))
        hop((0, 0), (-1, 0))
        hop((-sign, 0), (sign, 0))
        for dx in (0, 1, -1, 2):
            hop((dx, 0), (0, 1))
            hop((dx, 0), (0, -1))
            way = sign if dx in (0, 1) else -sign
            hop((dx, -way), (0, way))
    return plan


PLAN = send_plan()
RELAY = {1: (1, 2, 3, 4), 5: (5, 6, 7, 8, 9, 10), 8: (11, 12, 13, 14), 13: (15,)}


def split3(wide):
    hi = wide.astype(jnp.bfloat16)
    rest = wide - hi.astype(jnp.float32)
    mid = rest.astype(jnp.bfloat16)
    low = (rest - mid.astype(jnp.float32)).astype(jnp.bfloat16)
    return hi, mid, low


def attention_kernel(size_x, size_y, q_ref, k_ref, v_ref, o_ref, kbuf, vbuf, qw, kk, m_s, l_s, acc, sbuf,
                     send_sem, recv_k, recv_v):
    heads, head_dim, tokens = q_ref.shape
    num_kv = k_ref.shape[0] // head_dim
    group = heads // num_kv
    slots = len(SLOTS)
    cx, cy = lax.axis_index("cx"), lax.axis_index("cy")
    core = cx % 2
    chip_x = cx // 2

    def peer(step_x, step_y):
        return {"cx": ((chip_x + step_x + size_x) % size_x) * 2 + core, "cy": (cy + step_y + size_y) % size_y}

    sibling = {"cx": chip_x * 2 + (1 - core), "cy": cy}
    mesh_id = pl.DeviceIdType.MESH

    barrier = pltpu.get_barrier_semaphore()
    for device in (peer(1, 0), peer(-1, 0), peer(0, 1), peer(0, -1), sibling):
        pl.semaphore_signal(barrier, inc=1, device_id=device, device_id_type=mesh_id)
    pl.semaphore_wait(barrier, 5)

    bufs = {"k": (kbuf, recv_k, k_ref), "v": (vbuf, recv_v, v_ref)}
    copies = []

    def here(what, slot):
        buf, _, own = bufs[what]
        return own if slot == 0 else buf.at[slot, 0]

    def push(what, slot, dst_slot, plane, device):
        buf, recv, _ = bufs[what]
        copies.append((what, slot))
        pltpu.make_async_remote_copy(
            src_ref=here(what, slot), dst_ref=buf.at[dst_slot, plane], send_sem=send_sem.at[len(copies) - 1],
            recv_sem=recv.at[dst_slot, plane], device_id=device, device_id_type=mesh_id).start()

    def pass_on(what, slot):
        for step_x, step_y in PLAN.get((what, slot), ()):
            dx, dy = SLOTS[slot]
            push(what, slot, SLOT_OF[(wrap(dx - step_x), wrap(dy - step_y))], 0, peer(step_x, step_y))
        push(what, slot, slot, 1, sibling)

    def arrived(what, slot, plane):
        buf, recv, _ = bufs[what]
        pltpu.make_async_copy(buf.at[slot, plane], buf.at[slot, plane], recv.at[slot, plane]).wait()

    pass_on("k", 0)
    pass_on("v", 0)

    scale = math.log2(math.e) / math.sqrt(head_dim)
    for h in range(heads):
        hi, mid, low = split3(q_ref[h].astype(jnp.float32) * scale)
        qw[h, 0:head_dim] = hi
        qw[h, head_dim:2 * head_dim] = mid
        qw[h, 2 * head_dim:3 * head_dim] = low
        qw[h, 3 * head_dim:] = jnp.zeros_like(hi)
    m_s[...] = jnp.full(m_s.shape, -jnp.inf, jnp.float32)
    for ref in (l_s, acc):
        ref[...] = jnp.zeros(ref.shape, ref.dtype)
    vbuf[0, 0] = v_ref[...]

    def lay_out(slot, plane):
        own = slot == 0 and plane == 0
        for g in range(num_kv):
            part = slice(g * head_dim, (g + 1) * head_dim)
            kt = k_ref[part] if own else kbuf[slot, plane, part]
            kk[slot, g, plane] = jnp.concatenate([kt, kt], axis=0).T

    def make_ready(slot):
        for relay in RELAY.get(slot, ()):
            for what in ("k", "v"):
                arrived(what, relay, 0)
                pass_on(what, relay)
        for what in ("k", "v"):
            arrived(what, slot, 1)
        for plane in range(2):
            lay_out(slot, plane)

    def step(i, carry):
        for s in range(1, slots):
            @pl.when(i == s)
            def _():
                make_ready(s)
        tops = {}

        def scores(h, m):
            keys = kk[i, h // group, m]
            s = jnp.dot(jnp.concatenate([keys, keys], axis=1), qw[h], preferred_element_type=jnp.float32)
            sbuf[h % (LAG + 1), m * tokens:(m + 1) * tokens] = s
            top = jnp.max(s.reshape(tokens // 8, 8, tokens), axis=0)
            tops[h] = top if m == 0 else jnp.maximum(tops[h], top)

        for h in range(LAG):
            for m in range(2):
                scores(h, m)
        for h in range(heads):
            g = h // group
            m_prev = m_s[h]
            m_new = jnp.maximum(m_prev, jnp.max(tops[h], axis=0, keepdims=True))
            m_s[h] = m_new
            alpha = jnp.exp2(m_prev - m_new)
            total = l_s[h] * alpha
            out = (acc[h].reshape(head_dim // 8, 8, tokens) * alpha[None]).reshape(head_dim, tokens)
            for m in range(2):
                if h + LAG < heads:
                    scores(h + LAG, m)
                p = jnp.exp2(sbuf[h % (LAG + 1), m * tokens:(m + 1) * tokens].reshape(tokens // 8, 8, tokens) - m_new[None])
                total = total + jnp.sum(p, axis=0)
                out = out + jnp.dot(vbuf[i, m, g * head_dim:(g + 1) * head_dim],
                                    p.reshape(tokens, tokens).astype(jnp.bfloat16), preferred_element_type=jnp.float32)
            l_s[h] = total
            acc[h] = out
        return carry

    make_ready(0)
    lax.fori_loop(0, slots, step, 0)
    for h in range(heads):
        total = jnp.sum(l_s[h], axis=0, keepdims=True)
        o_ref[h] = (acc[h] / total).astype(jnp.bfloat16)
    for n, (what, slot) in enumerate(copies):
        pltpu.make_async_copy(here(what, slot), here(what, slot), send_sem.at[n]).wait()


def solution(mesh):
    size_x = mesh.shape["cx"] // 2
    size_y = mesh.shape["cy"]
    seq_spec = P(("batch", "cx", "cy"), None, None)

    def local_attention(q_local, k_local, v_local):
        tokens, heads, head_dim = q_local.shape
        num_kv = k_local.shape[1]
        q_t = jnp.transpose(q_local, (1, 2, 0))
        k_t = jnp.transpose(k_local, (1, 2, 0)).reshape(num_kv * head_dim, tokens)
        v_t = jnp.transpose(v_local, (1, 2, 0)).reshape(num_kv * head_dim, tokens)
        slots = len(SLOTS)
        f32, bf16 = jnp.float32, jnp.bfloat16
        out = pl.pallas_call(
            functools.partial(attention_kernel, size_x, size_y),
            out_shape=jax.ShapeDtypeStruct((heads, head_dim, tokens), bf16),
            in_specs=[pl.BlockSpec(memory_space=pltpu.VMEM)] * 3,
            out_specs=pl.BlockSpec(memory_space=pltpu.VMEM),
            scratch_shapes=[
                pltpu.VMEM((slots, 2, num_kv * head_dim, tokens), bf16),
                pltpu.VMEM((slots, 2, num_kv * head_dim, tokens), bf16),
                pltpu.VMEM((heads, 256, tokens), bf16),
                pltpu.VMEM((slots, num_kv, 2, tokens, 2 * head_dim), bf16),
                pltpu.VMEM((heads, 8, tokens), f32),
                pltpu.VMEM((heads, 8, tokens), f32),
                pltpu.VMEM((heads, head_dim, tokens), f32),
                pltpu.VMEM((LAG + 1, 2 * tokens, tokens), f32),
                pltpu.SemaphoreType.DMA((64,)),
                pltpu.SemaphoreType.DMA((slots, 2)),
                pltpu.SemaphoreType.DMA((slots, 2)),
            ],
            compiler_params=pltpu.CompilerParams(
                collective_id=0, has_side_effects=True, vmem_limit_bytes=48 * 2**20),
            name="attention",
        )(q_t, k_t, v_t)
        return jnp.transpose(out, (2, 0, 1))

    return jax.shard_map(local_attention, mesh=mesh, in_specs=(seq_spec, seq_spec, seq_spec), out_specs=seq_spec, check_vma=False)
```

time: 185 us -> 64.1 us (0.35)
  the two profiles are of different devices: /device:TPU:96 before, /device:TPU:97 now
where the time goes in v1:
time: 64.1 us; the launch traced here: 63.9 us
  Pallas kernels  60.5 us (94%)
  local copies, waits for them, and re-layouts  3.47 us (5%)
    pallas_call x1, Pallas kernels, local_attention(): pl.pallas_call(functools.partial(attention_kernel, size_x, size_y), out_s...  60.5 us
    unnamed x7, local copies, waits for them, and re-layouts  3.47 us

profile of v1, /device:TPU:97, one launch (start us, length us, event | category | flops | bytes accessed | tf_op | source)
XLA Modules:
  0.0 63.9 jit_solution(9631962072589499537)
XLA Ops:
  0.0 0.0 copy-start
  0.0 1.0 %copy-done = bf16[256,14,64]{0,2,1:T(8,128)(2,1)S(1)} copy-done((bf16[256,14,64]{0,2,1:T(8,128)(2,1)S(1)}, bf16[256,14,64]{0,2,1:T(8,128)(2,1)}, u32[]{:S(2)}) %copy-start) | copy-done | bytes 458776
  1.0 0.0 copy-start.1
  1.0 0.8 %copy-done.1 = bf16[256,2,64]{0,2,1:T(8,128)(2,1)S(1)} copy-done((bf16[256,2,64]{0,2,1:T(8,128)(2,1)S(1)}, bf16[256,2,64]{0,2,1:T(8,128)(2,1)}, u32[]{:S(2)}) %copy-start.1) | copy-done | bytes 65560
  1.9 0.0 copy-start.2
  1.9 0.8 %copy-done.2 = bf16[256,2,64]{0,2,1:T(8,128)(2,1)S(1)} copy-done((bf16[256,2,64]{0,2,1:T(8,128)(2,1)S(1)}, bf16[256,2,64]{0,2,1:T(8,128)(2,1)}, u32[]{:S(2)}) %copy-start.2) | copy-done | bytes 65560
  2.7 60.5 %attention.1 = bf16[14,64,256]{2,1,0:T(8,128)(2,1)S(1)} custom-call(bf16[14,64,256]{2,1,0:T(8,128)(2,1)S(1)} %bitcast.9, bf16[128,256]{1,0:T(8,128)(2,1)S(1)} %bitcast.10, bf16[128,256]{1,0:T(8,128)(2,1)S(1)} %bitcast.11), custom_call_target="tpu_custom_call" | custom-call | tf_op jit(solution)/shard_map/attention/pallas_call | solution.py:191
  63.2 0.8 %copy.5 = bf16[256,14,64]{0,2,1:T(8,128)(2,1)} copy(bf16[256,14,64]{0,2,1:T(8,128)(2,1)S(1)} %bitcast.8) | data formatting | bytes 917504
Async XLA Ops:
  0.0 1.0 %copy-start = (bf16[256,14,64]{0,2,1:T(8,128)(2,1)S(1)}, bf16[256,14,64]{0,2,1:T(8,128)(2,1)}, u32[]{:S(2)}) copy-start(bf16[256,14,64]{0,2,1:T(8,128)(2,1)} %param.3) | copy-start | bytes 1376260
  1.0 0.8 %copy-start.1 = (bf16[256,2,64]{0,2,1:T(8,128)(2,1)S(1)}, bf16[256,2,64]{0,2,1:T(8,128)(2,1)}, u32[]{:S(2)}) copy-start(bf16[256,2,64]{0,2,1:T(8,128)(2,1)} %param.4) | copy-start | bytes 196612
  1.9 0.8 %copy-start.2 = (bf16[256,2,64]{0,2,1:T(8,128)(2,1)S(1)}, bf16[256,2,64]{0,2,1:T(8,128)(2,1)}, u32[]{:S(2)}) copy-start(bf16[256,2,64]{0,2,1:T(8,128)(2,1)} %param.5) | copy-start | bytes 196612

commit v2 on v1

v2 whole, which is shorter than its diff:
```python
import functools
import math
import jax
import jax.numpy as jnp
from jax import lax
from jax.experimental import pallas as pl
from jax.experimental.pallas import tpu as pltpu
from jax.sharding import PartitionSpec as P

SLOTS = [(0, 0), (1, 0), (-1, 0), (0, 1), (0, -1), (1, 1), (1, -1), (-1, 1), (-1, -1), (2, 0), (0, 2),
         (2, 1), (2, -1), (1, 2), (-1, 2), (2, 2)]
SLOT_OF = {offset: slot for slot, offset in enumerate(SLOTS)}
LAG = 3
VALUE_LAG = 2
CHUNK = 64
DEPTH = 4


def wrap(step):
    return (step + 1) % 4 - 1


def send_plan():
    plan = {}

    def add(what, offset, step_x, step_y):
        plan.setdefault((what, SLOT_OF[offset]), []).append((step_x, step_y))

    for what, swap in (("k", False), ("v", True)):
        flip = (lambda pair: (pair[1], pair[0])) if swap else (lambda pair: pair)
        sign = -1 if swap else 1

        def hop(offset, step):
            add(what, flip(offset), *flip(step))

        hop((0, 0), (1, 0))
        hop((0, 0), (-1, 0))
        hop((-sign, 0), (sign, 0))
        for dx in (0, 1, -1, 2):
            hop((dx, 0), (0, 1))
            hop((dx, 0), (0, -1))
            way = sign if dx in (0, 1) else -sign
            hop((dx, -way), (0, way))
    return plan


PLAN = send_plan()
RELAY = {1: (1, 2, 3, 4), 5: (5, 6, 7, 8, 9, 10), 8: (11, 12, 13, 14), 13: (15,)}


def split3(wide):
    hi = wide.astype(jnp.bfloat16)
    rest = wide - hi.astype(jnp.float32)
    mid = rest.astype(jnp.bfloat16)
    low = (rest - mid.astype(jnp.float32)).astype(jnp.bfloat16)
    return hi, mid, low


def attention_kernel(size_x, size_y, q_hbm, k_hbm, v_hbm, o_ref, q_ref, kbuf, vbuf, qw, kk, m_s, l_s, acc, load_sem,
                     send_sem, recv_k, recv_v, *rings):
    heads, head_dim, tokens = q_ref.shape
    num_kv = kbuf.shape[2] // head_dim
    group = heads // num_kv
    slots = len(SLOTS)
    s_ring, p_ring = rings[:LAG + 1], rings[LAG + 1:]
    cx, cy = lax.axis_index("cx"), lax.axis_index("cy")
    core = cx % 2
    chip_x = cx // 2

    def peer(step_x, step_y):
        return {"cx": ((chip_x + step_x + size_x) % size_x) * 2 + core, "cy": (cy + step_y + size_y) % size_y}

    sibling = {"cx": chip_x * 2 + (1 - core), "cy": cy}
    mesh_id = pl.DeviceIdType.MESH

    loads = [pltpu.make_async_copy(src, dst, load_sem.at[n]) for n, (src, dst) in enumerate(
        ((k_hbm, kbuf.at[0, 0]), (v_hbm, vbuf.at[0, 0]), (q_hbm, q_ref)))]
    for load in loads:
        load.start()
    barrier = pltpu.get_barrier_semaphore()
    for device in (peer(1, 0), peer(-1, 0), peer(0, 1), peer(0, -1), sibling):
        pl.semaphore_signal(barrier, inc=1, device_id=device, device_id_type=mesh_id)
    pl.semaphore_wait(barrier, 5)

    bufs = {"k": (kbuf, recv_k), "v": (vbuf, recv_v)}
    copies = []

    def push(what, slot, dst_slot, plane, device):
        buf, recv = bufs[what]
        copies.append((what, slot))
        pltpu.make_async_remote_copy(
            src_ref=buf.at[slot, 0], dst_ref=buf.at[dst_slot, plane], send_sem=send_sem.at[len(copies) - 1],
            recv_sem=recv.at[dst_slot, plane], device_id=device, device_id_type=mesh_id).start()

    def pass_on(what, slot):
        for step_x, step_y in PLAN.get((what, slot), ()):
            dx, dy = SLOTS[slot]
            push(what, slot, SLOT_OF[(wrap(dx - step_x), wrap(dy - step_y))], 0, peer(step_x, step_y))
        push(what, slot, slot, 1, sibling)

    def arrived(what, slot, plane):
        buf, recv = bufs[what]
        pltpu.make_async_copy(buf.at[slot, plane], buf.at[slot, plane], recv.at[slot, plane]).wait()

    for what, load in zip(("k", "v"), loads):
        load.wait()
        pass_on(what, 0)
    loads[2].wait()

    scale = math.log2(math.e) / math.sqrt(head_dim)
    for h in range(heads):
        hi, mid, low = split3(q_ref[h].astype(jnp.float32) * scale)
        qw[h, 0:head_dim] = hi
        qw[h, head_dim:2 * head_dim] = mid
        qw[h, 2 * head_dim:3 * head_dim] = low
        qw[h, 3 * head_dim:] = jnp.zeros_like(hi)
    m_s[...] = jnp.full(m_s.shape, -jnp.inf, jnp.float32)
    for ref in (l_s, acc):
        ref[...] = jnp.zeros(ref.shape, ref.dtype)

    def step(i, carry):
        for s, relays in RELAY.items():
            @pl.when(i == s)
            def _():
                for relay in relays:
                    for what in ("k", "v"):
                        arrived(what, relay, 0)
                        pass_on(what, relay)
        for what in ("k", "v"):
            arrived(what, i, 1)
        for g in range(num_kv):
            for m in range(2):
                kt = kbuf[i, m, g * head_dim:(g + 1) * head_dim]
                kk[g, m] = jnp.concatenate([kt, kt], axis=0).T
        fill, drain = i // slots, 0
        tops, peaks, alphas, totals, outs, sums = {}, {}, {}, {}, {}, {}

        def scores(h, m):
            keys = kk[h // group, m]
            s = jnp.dot(jnp.concatenate([keys, keys], axis=1), qw[h], preferred_element_type=jnp.float32)
            s_ring[h % (LAG + 1)][fill, m * tokens:(m + 1) * tokens] = s
            top = jnp.max(s.reshape(tokens // 8, 8, tokens), axis=0)
            tops[h] = top if m == 0 else jnp.maximum(tops[h], top)

        def weights(h, m):
            if m == 0:
                m_prev = m_s[h]
                peaks[h] = jnp.maximum(m_prev, jnp.max(tops[h], axis=0, keepdims=True))
                m_s[h] = peaks[h]
                alphas[h] = jnp.exp2(m_prev - peaks[h])
                totals[h] = l_s[h] * alphas[h]
                sums[h] = []
            for r in range(0, tokens, CHUNK):
                peak = peaks[h]
                if len(sums[h]) >= DEPTH:
                    peak = jnp.maximum(peak, jnp.minimum(peak, sums[h][-DEPTH]))
                s = s_ring[h % (LAG + 1)][drain, m * tokens + r:m * tokens + r + CHUNK]
                p = jnp.exp2(s.reshape(CHUNK // 8, 8, tokens) - peak[None])
                totals[h] = totals[h] + jnp.sum(p, axis=0)
                sums[h].append(totals[h])
                p_ring[(2 * h + m) % len(p_ring)][fill, r:r + CHUNK] = p.reshape(CHUNK, tokens).astype(jnp.bfloat16)
            if m == 1:
                l_s[h] = totals[h]

        def values(h, m):
            g = h // group
            out = jnp.dot(vbuf[i, m, g * head_dim:(g + 1) * head_dim], p_ring[(2 * h + m) % len(p_ring)][drain],
                          preferred_element_type=jnp.float32)
            outs[h] = out if m == 0 else outs[h] + out
            if m == 1:
                old = acc[h].reshape(head_dim // 8, 8, tokens) * alphas[h][None]
                acc[h] = old.reshape(head_dim, tokens) + outs[h]

        for u in range(-2 * LAG, 2 * heads + VALUE_LAG):
            for offset, part in ((2 * LAG, scores), (0, weights), (-VALUE_LAG, values)):
                if 0 <= u + offset < 2 * heads:
                    part((u + offset) // 2, (u + offset) % 2)
        return carry

    lax.fori_loop(0, slots, step, 0)
    for h in range(heads):
        total = jnp.sum(l_s[h], axis=0, keepdims=True)
        o_ref[h] = (acc[h] / total).astype(jnp.bfloat16)
    for n, (what, slot) in enumerate(copies):
        buf, _ = bufs[what]
        pltpu.make_async_copy(buf.at[slot, 0], buf.at[slot, 0], send_sem.at[n]).wait()


def solution(mesh):
    size_x = mesh.shape["cx"] // 2
    size_y = mesh.shape["cy"]
    seq_spec = P(("batch", "cx", "cy"), None, None)

    def local_attention(q_local, k_local, v_local):
        tokens, heads, head_dim = q_local.shape
        num_kv = k_local.shape[1]
        q_t = jnp.transpose(q_local, (1, 2, 0))
        k_t = jnp.transpose(k_local, (1, 2, 0)).reshape(num_kv * head_dim, tokens)
        v_t = jnp.transpose(v_local, (1, 2, 0)).reshape(num_kv * head_dim, tokens)
        slots = len(SLOTS)
        f32, bf16 = jnp.float32, jnp.bfloat16
        out = pl.pallas_call(
            functools.partial(attention_kernel, size_x, size_y),
            out_shape=jax.ShapeDtypeStruct((heads, head_dim, tokens), bf16),
            in_specs=[pl.BlockSpec(memory_space=pltpu.HBM)] * 3,
            out_specs=pl.BlockSpec(memory_space=pltpu.VMEM),
            scratch_shapes=[
                pltpu.VMEM((heads, head_dim, tokens), bf16),
                pltpu.VMEM((slots, 2, num_kv * head_dim, tokens), bf16),
                pltpu.VMEM((slots, 2, num_kv * head_dim, tokens), bf16),
                pltpu.VMEM((heads, 256, tokens), bf16),
                pltpu.VMEM((num_kv, 2, tokens, 2 * head_dim), bf16),
                pltpu.VMEM((heads, 8, tokens), f32),
                pltpu.VMEM((heads, 8, tokens), f32),
                pltpu.VMEM((heads, head_dim, tokens), f32),
                pltpu.SemaphoreType.DMA((3,)),
                pltpu.SemaphoreType.DMA((64,)),
                pltpu.SemaphoreType.DMA((slots, 2)),
                pltpu.SemaphoreType.DMA((slots, 2)),
            ] + [pltpu.VMEM((2, 2 * tokens, tokens), f32)] * (LAG + 1) + [pltpu.VMEM((2, tokens, tokens), bf16)] * 4,
            compiler_params=pltpu.CompilerParams(
                collective_id=0, has_side_effects=True, vmem_limit_bytes=20 * 2**20),
            name="attention",
        )(*(pltpu.with_memory_space_constraint(x, pltpu.HBM) for x in (q_t, k_t, v_t)))
        return jnp.transpose(out, (2, 0, 1))

    return jax.shard_map(local_attention, mesh=mesh, in_specs=(seq_spec, seq_spec, seq_spec), out_specs=seq_spec, check_vma=False)
```

time: 64.1 us -> 46.7 us (0.73)
  Pallas kernels: 60.5 us -> 45.9 us
  local copies, waits for them, and re-layouts: 3.47 us -> 0.77 us
    pallas_call x1, Pallas kernels: 60.5 us -> 45.9 us  [local_attention(): pl.pallas_call(functools.partial(attention_kernel, size_x, size_y), out_s...]
    unnamed x7 -> x1, local copies, waits for them, and re-layouts: 3.47 us -> 0.77 us
where the time goes in v2:
time: 46.7 us
  Pallas kernels  45.9 us (98%)
  local copies, waits for them, and re-layouts  0.77 us (2%)
    pallas_call x1, Pallas kernels, local_attention(): pl.pallas_call(functools.partial(attention_kernel, size_x, size_y), out_s...  45.9 us

profile of v2, /device:TPU:97, one launch (start us, length us, event | category | flops | bytes accessed | tf_op | source)
XLA Modules:
  0.0 46.7 jit_solution(5215987382561071250)
XLA Ops:
  0.0 45.9 %attention.1 = bf16[14,64,256]{2,1,0:T(8,128)(2,1)S(1)} custom-call(bf16[14,64,256]{2,1,0:T(8,128)(2,1)} %bitcast.9, bf16[128,256]{1,0:T(8,128)(2,1)} %bitcast.10, bf16[128,256]{1,0:T(8,128)(2,1)} %bitcast.11), custom_call_target="tpu_custom_call" | custom-call | tf_op jit(solution)/shard_map/attention/pallas_call | solution.py:202
  45.9 0.8 %copy.5 = bf16[256,14,64]{0,2,1:T(8,128)(2,1)} copy(bf16[256,14,64]{0,2,1:T(8,128)(2,1)S(1)} %bitcast.8) | data formatting | bytes 917504

commit v3 on v2

--- a/solution.py
+++ b/solution.py
@@ -12,8 +12,8 @@
 SLOT_OF = {offset: slot for slot, offset in enumerate(SLOTS)}
 LAG = 3
 VALUE_LAG = 2
-CHUNK = 64
-DEPTH = 4
+CHUNK = 128
+DEPTH = 3
 
 
 def wrap(step):
@@ -45,7 +45,7 @@
 
 
 PLAN = send_plan()
-RELAY = {1: (1, 2, 3, 4), 5: (5, 6, 7, 8, 9, 10), 8: (11, 12, 13, 14), 13: (15,)}
+RELAY = {1: (1, 2, 3, 4), 4: (5, 6, 7, 8, 9, 10), 7: (11, 12, 13, 14), 12: (15,)}
 
 
 def split3(wide):

time: 46.7 us -> 43.8 us (0.938)
  Pallas kernels: 45.9 us -> 42.9 us
    pallas_call x1, Pallas kernels: 45.9 us -> 42.9 us  [local_attention(): pl.pallas_call(functools.partial(attention_kernel, size_x, size_y), out_s...]
where the time goes in v3:
time: 43.8 us; the launch traced here: 43.7 us
  Pallas kernels  42.9 us (98%)
  local copies, waits for them, and re-layouts  0.77 us (2%)
    pallas_call x1, Pallas kernels, local_attention(): pl.pallas_call(functools.partial(attention_kernel, size_x, size_y), out_s...  42.9 us

profile of v3, /device:TPU:97, one launch (start us, length us, event | category | flops | bytes accessed | tf_op | source)
XLA Modules:
  0.0 43.7 jit_solution(13015977726979583920)
XLA Ops:
  0.0 42.9 %attention.1 = bf16[14,64,256]{2,1,0:T(8,128)(2,1)S(1)} custom-call(bf16[14,64,256]{2,1,0:T(8,128)(2,1)} %bitcast.9, bf16[128,256]{1,0:T(8,128)(2,1)} %bitcast.10, bf16[128,256]{1,0:T(8,128)(2,1)} %bitcast.11), custom_call_target="tpu_custom_call" | custom-call | tf_op jit(solution)/shard_map/attention/pallas_call | solution.py:202
  42.9 0.8 %copy.5 = bf16[256,14,64]{0,2,1:T(8,128)(2,1)} copy(bf16[256,14,64]{0,2,1:T(8,128)(2,1)S(1)} %bitcast.8) | data formatting | bytes 917504
